TPU v7x, 16 devices: a whole 2x2x2 slice. The times are simulated.
16 devices in a mesh: dpy: 2 (over z), dpx: 2 (over y), tp: 4 (over x, core).
Axes of the slice: x: 2, y: 2, z: 2, core: 2. Of those that a mesh axis runs over, the one named last changes fastest.
Arguments:
- x_saved: bfloat16 [2, 128, 512, 512], P(None, ('dpy', 'dpx'))
- y_saved: bfloat16 [2, 128, 512, 512], P(None, ('dpy', 'dpx'))
- d_out: bfloat16 [128, 512, 512], P(('dpy', 'dpx'))
- w_qkv: bfloat16 [2, 512, 3, 16, 32], P(None, None, None, 'tp')
- w_out: bfloat16 [2, 16, 32, 512], P(None, 'tp')
- w_up: bfloat16 [2, 512, 2048], P(None, None, 'tp')
- w_down: bfloat16 [2, 2048, 512], P(None, 'tp')
Outputs:
- output 1: bfloat16 [128, 512, 512], P(('dpy', 'dpx'))
- output 2: float32 [2, 512, 3, 16, 32], P(None, None, None, 'tp')
- output 3: float32 [2, 16, 32, 512], P(None, 'tp')
- output 4: float32 [2, 512, 2048], P(None, None, 'tp')
- output 5: float32 [2, 2048, 512], P(None, 'tp')
All inputs are finite; a program needn't handle non-finite values.
Results may differ from a plain program's by a relative error of at most 0.02.
Values are sent between devices in bfloat16 or wider.
A program may use at most 1 GiB of HBM per device.

v0:
```python
import jax
import jax.numpy as jnp
from jax import lax
from jax.sharding import PartitionSpec as P

MICROBATCHES = 2


def layer_backward(x_in, y_mid, grad_out, wqkv_l, wout_l, wup_l, wdown_l):
    hidden = jnp.einsum('bsh,hf->bsf', y_mid, wup_l, preferred_element_type=jnp.float32)
    act_f32, gelu_pull = jax.vjp(jax.nn.gelu, hidden)
    act_b = act_f32.astype(jnp.bfloat16)
    g_down = jnp.einsum('bsf,bsh->fh', act_b, grad_out, preferred_element_type=jnp.float32)
    d_act = jnp.einsum('bsh,fh->bsf', grad_out, wdown_l, preferred_element_type=jnp.float32)
    d_hidden = gelu_pull(d_act)[0].astype(jnp.bfloat16)
    g_up = jnp.einsum('bsh,bsf->hf', y_mid, d_hidden, preferred_element_type=jnp.float32)
    mid_part = jnp.einsum('bsf,hf->bsh', d_hidden, wup_l, preferred_element_type=jnp.float32).astype(jnp.bfloat16)
    mid_sum = lax.psum(mid_part, 'tp')
    d_mid = (grad_out.astype(jnp.float32) + mid_sum.astype(jnp.float32)).astype(jnp.bfloat16)
    scale_factor = wqkv_l.shape[-1] ** -0.5
    queries = jnp.einsum('bsh,hnd->bsnd', x_in, wqkv_l[:, 0], preferred_element_type=jnp.float32).astype(jnp.bfloat16)
    keys_all = jnp.einsum('bsh,hnd->bsnd', x_in, wqkv_l[:, 1], preferred_element_type=jnp.float32).astype(jnp.bfloat16)
    values = jnp.einsum('bsh,hnd->bsnd', x_in, wqkv_l[:, 2], preferred_element_type=jnp.float32).astype(jnp.bfloat16)
    scores = jnp.einsum('bqnd,bknd->bnqk', queries, keys_all, preferred_element_type=jnp.float32) * scale_factor
    probs_f = jax.nn.softmax(scores, axis=-1)
    probs_b = probs_f.astype(jnp.bfloat16)
    att_out = jnp.einsum('bnqk,bknd->bqnd', probs_b, values, preferred_element_type=jnp.float32).astype(jnp.bfloat16)
    d_att = jnp.einsum('bsh,ndh->bsnd', d_mid, wout_l, preferred_element_type=jnp.float32).astype(jnp.bfloat16)
    g_out = jnp.einsum('bsnd,bsh->ndh', att_out, d_mid, preferred_element_type=jnp.float32)
    d_probs = jnp.einsum('bqnd,bknd->bnqk', d_att, values, preferred_element_type=jnp.float32)
    d_values = jnp.einsum('bnqk,bqnd->bknd', probs_b, d_att, preferred_element_type=jnp.float32).astype(jnp.bfloat16)
    row_dot = jnp.sum(d_probs * probs_f, axis=-1, keepdims=True)
    d_scores = (probs_f * (d_probs - row_dot) * scale_factor).astype(jnp.bfloat16)
    d_queries = jnp.einsum('bnqk,bknd->bqnd', d_scores, keys_all, preferred_element_type=jnp.float32).astype(jnp.bfloat16)
    d_keys = jnp.einsum('bnqk,bqnd->bknd', d_scores, queries, preferred_element_type=jnp.float32).astype(jnp.bfloat16)
    d_qkv = jnp.stack([d_queries, d_keys, d_values], axis=2)
    g_qkv = jnp.einsum('bsh,bscnd->hcnd', x_in, d_qkv, preferred_element_type=jnp.float32)
    in_part = jnp.einsum('bscnd,hcnd->bsh', d_qkv, wqkv_l, preferred_element_type=jnp.float32).astype(jnp.bfloat16)
    in_sum = lax.psum(in_part, 'tp')
    d_in = (d_mid.astype(jnp.float32) + in_sum.astype(jnp.float32)).astype(jnp.bfloat16)
    return d_in, (g_qkv, g_out, g_up, g_down)


def solution(mesh):
    data_axes = ('dpy', 'dpx')
    replicas = mesh.shape['dpy'] * mesh.shape['dpx']
    act_spec = P(None, data_axes, None, None)
    tok_spec = P(data_axes, None, None)
    qkv_spec = P(None, None, None, 'tp', None)
    wout_spec = P(None, 'tp', None, None)
    up_spec = P(None, None, 'tp')
    down_spec = P(None, 'tp', None)

    def device_backward(x_saved, y_saved, d_out, w_qkv, w_out, w_up, w_down):
        num_layers = w_qkv.shape[0]
        micro_rows = d_out.shape[0] // MICROBATCHES
        grad_acc = [None] * num_layers
        d_inputs = []
        for micro_idx in range(MICROBATCHES):
            row_range = slice(micro_idx * micro_rows, (micro_idx + 1) * micro_rows)
            grad_cur = d_out[row_range]
            for layer_idx in reversed(range(num_layers)):
                grad_cur, grads_new = layer_backward(x_saved[layer_idx, row_range], y_saved[layer_idx, row_range], grad_cur, w_qkv[layer_idx], w_out[layer_idx], w_up[layer_idx], w_down[layer_idx])
                if micro_idx == 0:
                    grad_acc[layer_idx] = grads_new
                else:
                    grad_acc[layer_idx] = tuple(grad_prev + grad_next for grad_prev, grad_next in zip(grad_acc[layer_idx], grads_new))
                if micro_idx == MICROBATCHES - 1:
                    grad_acc[layer_idx] = tuple(lax.psum(grad_sum, data_axes) / replicas for grad_sum in grad_acc[layer_idx])
            d_inputs.append(grad_cur)
        stacked = tuple(jnp.stack([grad_set[slot_idx] for grad_set in grad_acc]) for slot_idx in range(4))
        return (jnp.concatenate(d_inputs, axis=0),) + stacked

    return jax.shard_map(device_backward, mesh=mesh, in_specs=(act_spec, act_spec, tok_spec, qkv_spec, wout_spec, up_spec, down_spec), out_specs=(tok_spec, qkv_spec, wout_spec, up_spec, down_spec), check_vma=False)
```

profile of v0, /device:TPU:0, one launch (start us, length us, event | category | flops | bytes accessed | tf_op | source)
XLA Modules:
  0.0 2527.9 jit_solution(11172296990226737745)
XLA Ops:
  231.6 29.3 %fusion.509 = (f32[16,4,512]{2,1,0:T(4,128)S(1)}, f32[16,4,512,512]{2,3,1,0:T(8,128)}) fusion(bf16[16,512,4,32]{1,3,2,0:T(8,128)(2,1)} %fusion.261, bf16[16,512,4,32]{1,3,2,0:T(8,128)(2,1)} %fusion.258), kind=kOutput, calls=%fused_computation.392 | convolution fusion | flops 1124073984 | bytes 71434240 | tf_op jit(solution)/shard_map/sub | solution.py:25
  261.6 32.9 %fusion.504 = bf16[16,4,512,512]{2,3,1,0:T(8,128)(2,1)} fusion(f32[16,4,512,512]{2,3,1,0:T(8,128)} %get-tuple-element.33, f32[16,4,512]{2,1,0:T(4,128)S(1)} %get-tuple-element.32), kind=kLoop, calls=%fused_computation.387 | loop fusion | flops 33554432 | bytes 100794368 | tf_op jit(solution)/shard_map/convert_element_type | solution.py:26
  294.5 28.5 %fusion.508 = (f32[16,4,512]{2,1,0:T(4,128)S(1)}, f32[16,4,512,512]{2,3,1,0:T(8,128)}) fusion(bf16[16,512,4,32]{1,3,2,0:T(8,128)(2,1)} %fusion.279, bf16[16,512,4,32]{1,3,2,0:T(8,128)(2,1)S(1)} %copy-done.45), kind=kOutput, calls=%fused_computation.391 | convolution fusion | flops 1124073984 | bytes 71434240 | tf_op jit(solution)/shard_map/sub | solution.py:25
  323.6 32.9 %fusion.506 = bf16[16,4,512,512]{2,3,1,0:T(8,128)(2,1)} fusion(f32[16,4,512,512]{2,3,1,0:T(8,128)} %get-tuple-element.31, f32[16,4,512]{2,1,0:T(4,128)S(1)} %get-tuple-element.30), kind=kLoop, calls=%fused_computation.389 | loop fusion | flops 33554432 | bytes 100794368 | tf_op jit(solution)/shard_map/convert_element_type | solution.py:26
  356.5 28.7 %fusion.511 = (f32[16,4,512]{2,1,0:T(4,128)S(1)}, f32[16,4,512,512]{2,3,1,0:T(8,128)}) fusion(bf16[16,512,4,32]{1,3,2,0:T(8,128)(2,1)} %fusion.270, bf16[16,512,4,32]{1,3,2,0:T(8,128)(2,1)S(1)} %copy-done.43), kind=kOutput, calls=%fused_computation.394 | convolution fusion | flops 1124073984 | bytes 71434240 | tf_op jit(solution)/shard_map/sub | solution.py:25
  385.9 32.9 %fusion.505 = bf16[16,4,512,512]{2,3,1,0:T(8,128)(2,1)} fusion(f32[16,4,512,512]{2,3,1,0:T(8,128)} %get-tuple-element.37, f32[16,4,512]{2,1,0:T(4,128)S(1)} %get-tuple-element.36), kind=kLoop, calls=%fused_computation.388 | loop fusion | flops 33554432 | bytes 100794368 | tf_op jit(solution)/shard_map/convert_element_type | solution.py:26
  418.8 28.8 %fusion.510 = (f32[16,4,512]{2,1,0:T(4,128)S(1)}, f32[16,4,512,512]{2,3,1,0:T(8,128)}) fusion(bf16[16,512,4,32]{1,3,2,0:T(8,128)(2,1)} %fusion.288, bf16[16,512,4,32]{1,3,2,0:T(8,128)(2,1)S(1)} %copy-done.41), kind=kOutput, calls=%fused_computation.393 | convolution fusion | flops 1124073984 | bytes 71434240 | tf_op jit(solution)/shard_map/sub | solution.py:25
  458.9 32.7 %fusion.507 = bf16[16,4,512,512]{2,3,1,0:T(8,128)(2,1)} fusion(f32[16,4,512,512]{2,3,1,0:T(8,128)} %get-tuple-element.35, f32[16,4,512]{2,1,0:T(4,128)S(1)} %get-tuple-element.34), kind=kLoop, calls=%fused_computation.390 | loop fusion | flops 33554432 | bytes 100794368 | tf_op jit(solution)/shard_map/convert_element_type | solution.py:26
  515.6 23.2 fusion.512
  538.8 82.2 %convert_bitcast_fusion.10 = bf16[16,512,1,4,32]{1,4,3,0,2:T(8,128)(2,1)} fusion(bf16[16,512,4,32]{1,3,2,0:T(8,128)(2,1)S(1)} %copy-done.46, f32[16,4,512,512]{2,3,1,0:T(8,128)} %fusion.512, f32[16,4,512,512]{2,3,1,0:T(8,128)} %get-tuple-element.33, f32[16,4,512]{2,1,0:T(4,128)S(1)} %copy-done.38), kind=kOutput, calls=%fused_computation.239 | convolution fusion | flops 1192264192 | bytes 138543104 | tf_op jit(solution)/shard_map/bnqk,bqnd->bknd/dot_general | solution.py:35
  620.9 83.6 %convert_bitcast_fusion.11 = bf16[16,512,1,4,32]{1,4,3,0,2:T(8,128)(2,1)} fusion(bf16[16,512,4,32]{1,3,2,0:T(8,128)(2,1)} %fusion.258, f32[16,4,512,512]{2,3,1,0:T(8,128)} %fusion.512, f32[16,4,512,512]{2,3,1,0:T(8,128)} %get-tuple-element.33, f32[16,4,512]{2,1,0:T(4,128)S(1)} %copy-done.38), kind=kOutput, calls=%fused_computation.240 | convolution fusion | flops 1192264192 | bytes 138543104 | tf_op jit(solution)/shard_map/bnqk,bknd->bqnd/dot_general | solution.py:34
  735.3 83.4 %convert_bitcast_fusion.4 = bf16[16,512,1,4,32]{1,4,3,0,2:T(8,128)(2,1)} fusion(bf16[16,512,4,32]{1,3,2,0:T(8,128)(2,1)} %fusion.279, f32[16,4,512,512]{2,3,1,0:T(8,128)} %fusion.514, f32[16,4,512,512]{2,3,1,0:T(8,128)} %get-tuple-element.31, f32[16,4,512]{2,1,0:T(4,128)S(1)} %copy-done.36), kind=kOutput, calls=%fused_computation.233 | convolution fusion | flops 1192264192 | bytes 138543104 | tf_op jit(solution)/shard_map/bnqk,bqnd->bknd/dot_general | solution.py:35
  818.6 83.4 %convert_bitcast_fusion.5 = bf16[16,512,1,4,32]{1,4,3,0,2:T(8,128)(2,1)} fusion(bf16[16,512,4,32]{1,3,2,0:T(8,128)(2,1)} %fusion.276, f32[16,4,512,512]{2,3,1,0:T(8,128)} %fusion.514, f32[16,4,512,512]{2,3,1,0:T(8,128)} %get-tuple-element.31, f32[16,4,512]{2,1,0:T(4,128)S(1)} %copy-done.36), kind=kOutput, calls=%fused_computation.234 | convolution fusion | flops 1192264192 | bytes 138543104 | tf_op jit(solution)/shard_map/bnqk,bknd->bqnd/dot_general | solution.py:34
  1005.5 228.5 %all-reduce.17.cloned.1.call-done = (bf16[16,512,512]{2,1,0:T(8,128)(2,1)}, bf16[16,512,512]{2,1,0:T(8,128)(2,1)}) async-done(((bf16[16,512,512]{2,1,0:T(8,128)(2,1)}, bf16[16,512,512]{2,1,0:T(8,128)(2,1)}), (bf16[16,512,512]{2,1,0:T(8,128)(2,1)}, bf16[16,512,512]{2,1,0:T(8,128)(2,1)})) %all-reduce.17.cloned.1.call-update) | async-done | bytes 16777232 | tf_op jit(solution)/shard_map/psum | solution.py:39
  1234.0 23.4 fusion.95
  1267.7 23.6 fusion.81
  1367.7 218.4 %all-reduce.15.cloned.1.call-done = (bf16[16,512,512]{2,1,0:T(8,128)(2,1)}, bf16[16,512,512]{2,1,0:T(8,128)(2,1)}) async-done(((bf16[16,512,512]{2,1,0:T(8,128)(2,1)}, bf16[16,512,512]{2,1,0:T(8,128)(2,1)}), (bf16[16,512,512]{2,1,0:T(8,128)(2,1)}, bf16[16,512,512]{2,1,0:T(8,128)(2,1)})) %all-reduce.15.cloned.1.call-update) | async-done | bytes 16777232 | tf_op jit(solution)/shard_map/psum | solution.py:18
  1638.3 83.8 %convert_bitcast_fusion.7 = bf16[16,512,1,4,32]{1,4,3,0,2:T(8,128)(2,1)} fusion(bf16[16,512,4,32]{1,3,2,0:T(8,128)(2,1)} %fusion.270, f32[16,4,512,512]{2,3,1,0:T(8,128)} %fusion.513, f32[16,4,512,512]{2,3,1,0:T(8,128)} %get-tuple-element.37, f32[16,4,512]{2,1,0:T(4,128)S(1)} %copy-done.34), kind=kOutput, calls=%fused_computation.236 | convolution fusion | flops 1192264192 | bytes 138543104 | tf_op jit(solution)/shard_map/bnqk,bqnd->bknd/dot_general | solution.py:35
  1722.1 83.1 %convert_bitcast_fusion.8 = bf16[16,512,1,4,32]{1,4,3,0,2:T(8,128)(2,1)} fusion(bf16[16,512,4,32]{1,3,2,0:T(8,128)(2,1)S(1)} %copy-done.44, f32[16,4,512,512]{2,3,1,0:T(8,128)} %fusion.513, f32[16,4,512,512]{2,3,1,0:T(8,128)} %get-tuple-element.37, f32[16,4,512]{2,1,0:T(4,128)S(1)} %copy-done.34), kind=kOutput, calls=%fused_computation.237 | convolution fusion | flops 1192264192 | bytes 138543104 | tf_op jit(solution)/shard_map/bnqk,bknd->bqnd/dot_general | solution.py:34
  1845.3 23.1 fusion.515
  1868.5 82.1 %convert_bitcast_fusion.1 = bf16[16,512,1,4,32]{1,4,3,0,2:T(8,128)(2,1)} fusion(bf16[16,512,4,32]{1,3,2,0:T(8,128)(2,1)S(1)} %copy-done.42, f32[16,4,512,512]{2,3,1,0:T(8,128)} %fusion.515, f32[16,4,512,512]{2,3,1,0:T(8,128)} %get-tuple-element.35, f32[16,4,512]{2,1,0:T(4,128)S(1)} %copy-done.32), kind=kOutput, calls=%fused_computation.230 | convolution fusion | flops 1192264192 | bytes 138543104 | tf_op jit(solution)/shard_map/bnqk,bqnd->bknd/dot_general | solution.py:35
  1950.6 83.5 %convert_bitcast_fusion.2 = bf16[16,512,1,4,32]{1,4,3,0,2:T(8,128)(2,1)} fusion(bf16[16,512,4,32]{1,3,2,0:T(8,128)(2,1)} %fusion.285, f32[16,4,512,512]{2,3,1,0:T(8,128)} %fusion.515, f32[16,4,512,512]{2,3,1,0:T(8,128)} %get-tuple-element.35, f32[16,4,512]{2,1,0:T(4,128)S(1)} %copy-done.32), kind=kOutput, calls=%fused_computation.231 | convolution fusion | flops 1192264192 | bytes 138543104 | tf_op jit(solution)/shard_map/bnqk,bknd->bqnd/dot_general | solution.py:34
  2100.6 113.1 %all-reduce.11.cloned.1.call-done = (f32[512,3,4,32]{0,3,2,1:T(8,128)}, f32[512,3,4,32]{0,3,2,1:T(8,128)}, f32[4,32,512]{2,1,0:T(8,128)}, f32[4,32,512]{2,1,0:T(...) async-done(((f32[512,3,4,32]{0,3,2,1:T(8,128)}, f32[512,3,4,32]{0,3,2,1:T(8,128)}, f32[4,32,512]{2,1,0:T(8,128)}, ...) | async-done | bytes 6291472 | tf_op jit(solution)/shard_map/psum | solution.py:69
  2226.6 274.0 %all-reduce.13.cloned.1.call-done = (bf16[16,512,512]{2,1,0:T(8,128)(2,1)}, bf16[16,512,512]{2,1,0:T(8,128)(2,1)}) async-done(((bf16[16,512,512]{2,1,0:T(8,128)(2,1)}, bf16[16,512,512]{2,1,0:T(8,128)(2,1)}), (bf16[16,512,512]{2,1,0:T(8,128)(2,1)}, bf16[16,512,512]{2,1,0:T(8,128)(2,1)})) %all-reduce.13.cloned.1.call-update) | async-done | bytes 16777232 | tf_op jit(solution)/shard_map/psum | solution.py:39
  (215 shorter events, 674.4 us)
Async XLA Ops:
  7.2 484.5 %all-reduce.19.cloned.1.call-start = ((), (), s32[]{:S(2)}) async-start(), calls=%async_computation.4 | async-start | bytes 33554432 | tf_op jit(solution)/shard_map/psum | solution.py:18
  92.2 1141.8 %all-reduce.17.cloned.1.call-start = ((), (), s32[]{:S(2)}) async-start(), calls=%async_computation.3 | async-start | bytes 33554432 | tf_op jit(solution)/shard_map/psum | solution.py:39
  195.6 28.1 %slice-start.2 = ((s8[8388608]{0:T(1024)(128)(4,1)}), s8[4194304]{0:T(1024)(128)(4,1)S(1)}, s32[]{:S(2)}) async-start(s8[8388608]{0:T(1024)(128)(4,1)} %bitcast.524), calls=%async_computation.7 | async-start | bytes 8388608
  261.6 32.9 %copy-start.45 = (bf16[16,512,4,32]{1,3,2,0:T(8,128)(2,1)S(1)}, bf16[16,512,4,32]{1,3,2,0:T(8,128)(2,1)}, u32[]{:S(2)}) copy-start(bf16[16,512,4,32]{1,3,2,0:T(8,128)(2,1)} %fusion.276) | copy-start | bytes 6291460
  323.6 32.9 %copy-start.43 = (bf16[16,512,4,32]{1,3,2,0:T(8,128)(2,1)S(1)}, bf16[16,512,4,32]{1,3,2,0:T(8,128)(2,1)}, u32[]{:S(2)}) copy-start(bf16[16,512,4,32]{1,3,2,0:T(8,128)(2,1)} %fusion.267) | copy-start | bytes 6291460
  385.9 32.9 %copy-start.41 = (bf16[16,512,4,32]{1,3,2,0:T(8,128)(2,1)S(1)}, bf16[16,512,4,32]{1,3,2,0:T(8,128)(2,1)}, u32[]{:S(2)}) copy-start(bf16[16,512,4,32]{1,3,2,0:T(8,128)(2,1)} %fusion.285) | copy-start | bytes 6291460
  418.8 28.8 %copy-start.48 = (f32[512,512]{1,0:T(8,128)S(1)}, f32[512,512]{1,0:T(8,128)}, u32[]{:S(2)}) copy-start(f32[512,512]{1,0:T(8,128)} %fusion.332) | copy-start | bytes 3145732
  447.6 44.0 %copy-start.31 = (f32[16,4,512]{2,1,0:T(4,128)}, f32[16,4,512]{2,1,0:T(4,128)S(1)}, u32[]{:S(2)}) copy-start(f32[16,4,512]{2,1,0:T(4,128)S(1)} %get-tuple-element.34) | copy-start | bytes 393220
  491.7 23.9 copy-start.16
  515.6 23.2 copy-start.38
  515.6 23.2 copy-start.46
  620.9 83.6 %copy-start.22 = (bf16[2,4,32,512]{3,2,1,0:T(8,128)(2,1)S(1)}, bf16[2,4,32,512]{3,2,1,0:T(8,128)(2,1)}, u32[]{:S(2)}) copy-start(bf16[2,4,32,512]{3,2,1,0:T(8,128)(2,1)} %param.11) | copy-start | bytes 786436
  620.9 91.2 %copy-start.14 = (bf16[16,512,4,32]{1,3,2,0:T(8,128)(2,1)S(1)}, bf16[16,512,4,32]{1,3,2,0:T(8,128)(2,1)}, u32[]{:S(2)}) copy-start(bf16[16,512,4,32]{1,3,2,0:T(8,128)(2,1)} %fusion.282) | copy-start | bytes 6291460
  818.6 83.4 %copy-start.3 = (bf16[16,512,4,32]{1,3,2,0:T(8,128)(2,1)S(1)}, bf16[16,512,4,32]{1,3,2,0:T(8,128)(2,1)}, u32[]{:S(2)}) copy-start(bf16[16,512,4,32]{1,3,2,0:T(8,128)(2,1)} %copy-done.2) | copy-start | bytes 6291460
  946.7 639.4 %all-reduce.15.cloned.1.call-start = ((), (), s32[]{:S(2)}) async-start(), calls=%async_computation.2 | async-start | bytes 33554432 | tf_op jit(solution)/shard_map/psum | solution.py:18
  989.9 244.1 %copy-start.40 = (bf16[2,512,512]{2,1,0:T(8,128)(2,1)S(1)}, bf16[2,512,512]{2,1,0:T(8,128)(2,1)}, u32[]{:S(2)}) copy-start(bf16[2,512,512]{2,1,0:T(8,128)(2,1)} %param.13) | copy-start | bytes 3145732
  1234.0 23.4 copy-start.11
  1301.5 912.2 %all-reduce.11.cloned.1.call-start = ((), (), s32[]{:S(2)}) async-start(), calls=%async_computation | async-start | bytes 12582912 | tf_op jit(solution)/shard_map/psum | solution.py:69
  1586.1 24.9 copy-start.23
  1586.1 29.1 %copy-start.13 = (bf16[16,512,4,32]{1,3,2,0:T(8,128)(2,1)S(1)}, bf16[16,512,4,32]{1,3,2,0:T(8,128)(2,1)}, u32[]{:S(2)}) copy-start(bf16[16,512,4,32]{1,3,2,0:T(8,128)(2,1)} %fusion.273) | copy-start | bytes 6291460
  1638.3 83.8 %copy-start.44 = (bf16[16,512,4,32]{1,3,2,0:T(8,128)(2,1)S(1)}, bf16[16,512,4,32]{1,3,2,0:T(8,128)(2,1)}, u32[]{:S(2)}) copy-start(bf16[16,512,4,32]{1,3,2,0:T(8,128)(2,1)} %fusion.267) | copy-start | bytes 6291460
  1821.5 23.8 copy-start.12
  1950.6 83.5 %copy-start.9 = (bf16[16,512,4,32]{1,3,2,0:T(8,128)(2,1)S(1)}, bf16[16,512,4,32]{1,3,2,0:T(8,128)(2,1)}, u32[]{:S(2)}) copy-start(bf16[16,512,4,32]{1,3,2,0:T(8,128)(2,1)} %copy-done.8) | copy-start | bytes 6291460
  2083.1 417.5 %all-reduce.13.cloned.1.call-start = ((), (), s32[]{:S(2)}) async-start(), calls=%async_computation.1 | async-start | bytes 33554432 | tf_op jit(solution)/shard_map/psum | solution.py:39
  (46 other events, 478.0 us)
Sparse Core Ops, SparseCore 0:
  92.3 287.1 all-reduce.18
  946.8 287.1 all-reduce.16
  1301.6 284.3 all-reduce.14
  2083.2 130.4 all-reduce.10
  2216.1 284.3 all-reduce.12
where the time goes:
time: 2530 us
  matrix products  1460 us (58%)
  waiting for transfers between devices  834 us (33%)
  other arithmetic  199 us (8%)
    psum x2, waiting for transfers between devices, layer_backward(): in_sum = lax.psum(in_part, 'tp')  502 us
    dot_general x4, matrix products, layer_backward(): jnp.einsum('bnqk,bknd->bqnd', d_scores, keys_all, preferred_element_type=...  334 us
    dot_general x4, matrix products, layer_backward(): jnp.einsum('bnqk,bqnd->bknd', d_scores, queries, preferred_element_type=j...  332 us
    psum x2, waiting for transfers between devices, layer_backward(): mid_sum = lax.psum(mid_part, 'tp')  218 us
    convert_element_type x4, other arithmetic, layer_backward(): probs_b = probs_f.astype(jnp.bfloat16)  131 us
    sub x4, matrix products, layer_backward(): probs_f = jax.nn.softmax(scores, axis=-1)  115 us
    psum x1, waiting for transfers between devices, device_backward(): lax.psum(grad_sum, data_axes) / replicas  113 us
    dot_general x4, matrix products, layer_backward(): jnp.einsum('bqnd,bknd->bnqk', d_att, values, preferred_element_type=jnp.f...  92.6 us
  transfers between devices with their start and end apart: 5, of which 4 were waited for; matrix products, arithmetic and copies ran while one was open for 22% of the time, Pallas kernels for 0%

commit v1 on v0

v1 whole, which is shorter than its diff:
```python
import functools

import jax
import jax.numpy as jnp
from jax import lax
from jax.experimental import pallas as pl
from jax.experimental.pallas import tpu as pltpu
from jax.sharding import PartitionSpec as P

F32 = jnp.float32
BF16 = jnp.bfloat16
LOG2E = 1.4426950408889634
GELU_C = 0.7978845608028654
GELU_K = 0.044715


def dot_nn(a, b):
    return lax.dot_general(a, b, (((1,), (0,)), ((), ())), preferred_element_type=F32)


def dot_nt(a, b):
    return lax.dot_general(a, b, (((1,), (1,)), ((), ())), preferred_element_type=F32)


def gelu_pair(h, da):
    h2 = h * h
    th = jnp.tanh(h * (GELU_C + (GELU_C * GELU_K) * h2))
    q = 0.5 + 0.5 * th
    act = h * q
    slope = (2.0 * GELU_C) + (6.0 * GELU_C * GELU_K) * h2
    dh = da * (q + act * ((1.0 - q) * slope))
    return act.astype(BF16), dh.astype(BF16)


def mlp_kernel(*refs):
    y_ref, g_ref = refs[0:2]
    up_refs, down_refs = refs[2:6], refs[6:10]
    gy_ref = refs[10]
    gup_refs, gdown_refs = refs[11:15], refs[15:19]
    upt_ref, yt_ref, dht_ref, acc_ref = refs[19:23]
    step = pl.program_id(0)

    @pl.when(step == 0)
    def _():
        for j in range(4):
            upt_ref[j] = up_refs[j][...].T
            gup_refs[j][...] = jnp.zeros_like(gup_refs[j])
            gdown_refs[j][...] = jnp.zeros_like(gdown_refs[j])

    y = y_ref[0]
    g = g_ref[0]
    yt_ref[...] = y.T
    blocks = [(j, k) for j in range(4) for k in range(2)]
    sub = 256

    def first(j, k):
        rows = slice(k * sub, (k + 1) * sub)
        return dot_nt(upt_ref[j, rows, :], y), dot_nt(down_refs[j][rows, :], g)

    held = first(*blocks[0])
    for i, (j, k) in enumerate(blocks):
        rows = slice(k * sub, (k + 1) * sub)
        nxt = first(*blocks[i + 1]) if i + 1 < len(blocks) else None
        at, dht = gelu_pair(*held)
        dht_ref[j, rows, :] = dht
        gdown_refs[j][rows, :] += dot_nn(at, g)
        gup_refs[j][:, rows] += dot_nt(yt_ref[...], dht)
        if k == 1:
            part = dot_nn(up_refs[j][...], dht_ref[j])
            if j == 0:
                acc_ref[...] = part
            else:
                acc_ref[...] += part
        held = nxt
    gy_ref[0] = (g.astype(F32) + acc_ref[...].T).astype(BF16)


def mlp_call(y, g, ups, downs):
    seqs, length, width = y.shape
    row = pl.BlockSpec((1, length, width), lambda s: (s, 0, 0))
    full = pl.BlockSpec((width, width), lambda s: (0, 0))
    grad = jax.ShapeDtypeStruct((width, width), F32)
    outs = pl.pallas_call(
        mlp_kernel,
        grid=(seqs,),
        in_specs=[row, row] + [full] * 8,
        out_specs=[row] + [full] * 8,
        out_shape=[jax.ShapeDtypeStruct(y.shape, BF16)] + [grad] * 8,
        scratch_shapes=[
            pltpu.VMEM((4, width, width), BF16),
            pltpu.VMEM((width, length), BF16),
            pltpu.VMEM((4, width, length), BF16),
            pltpu.VMEM((width, length), F32),
        ],
        compiler_params=pltpu.CompilerParams(
            dimension_semantics=("arbitrary",), vmem_limit_bytes=60 * 1024 * 1024
        ),
        cost_estimate=pl.CostEstimate(
            flops=10 * seqs * length * width * 4 * width, bytes_accessed=40 * 1024 * 1024, transcendentals=0
        ),
        name="mlp_bwd",
    )(y, g, *ups, *downs)
    return outs[0], outs[1:5], outs[5:9]


def att_kernel(heads, *refs):
    x_ref, gy_ref = refs[0:2]
    qkv_refs, out_refs = refs[2:6], refs[6:10]
    gx_ref = refs[10]
    gqkv_refs, gout_refs = refs[11:15], refs[15:19]
    wq_ref, wqt_ref, wo_ref, dqkv_ref, ot_ref, acc_ref, gq_ref, go_ref = refs[19:27]
    seq, grp = pl.program_id(0), pl.program_id(1)
    width = x_ref.shape[2]
    group = heads * 32

    @pl.when(jnp.logical_and(seq == 0, grp == 0))
    def _():
        for j in range(4):
            wq_ref[j] = qkv_refs[j][...]
            wqt_ref[j] = qkv_refs[j][...].T
            wo_ref[j] = out_refs[j][...]
        gq_ref[...] = jnp.zeros_like(gq_ref)
        go_ref[...] = jnp.zeros_like(go_ref)

    x = x_ref[0]
    gy = gy_ref[0]
    qkvt = dot_nt(wqt_ref[grp], x).astype(BF16)
    dot_ = dot_nt(wo_ref[grp], gy).astype(BF16)
    qt, kt, vt = qkvt[0:group], qkvt[group : 2 * group], qkvt[2 * group :]
    keys, values = kt.T, vt.T
    scale = 32 ** -0.5
    head_of = lax.broadcasted_iota(jnp.int32, qt.shape, 0) // 32

    def scores(n):
        own = head_of == n
        zero = jnp.zeros_like(qt)
        return dot_nn(keys, jnp.where(own, qt, zero)), dot_nn(values, jnp.where(own, dot_, zero))

    held = scores(0)
    for n in range(heads):
        rows = slice(32 * n, 32 * n + 32)
        nxt = scores(n + 1) if n + 1 < heads else None
        st, dpt = held
        top = jnp.max(st, axis=0, keepdims=True)
        e = jnp.exp2((st - top) * (scale * LOG2E))
        inv = 1.0 / jnp.sum(e, axis=0, keepdims=True)
        delta = jnp.sum(e * dpt, axis=0, keepdims=True) * inv
        pt = (e * inv).astype(BF16)
        dst = ((e * (inv * scale)) * (dpt - delta)).astype(BF16)
        ot_ref[rows] = dot_nn(vt[rows], pt).astype(BF16)
        dqkv_ref[2 * group + 32 * n : 2 * group + 32 * n + 32] = dot_nt(dot_[rows], pt).astype(BF16)
        dqkv_ref[rows] = dot_nn(kt[rows], dst).astype(BF16)
        dqkv_ref[group + 32 * n : group + 32 * n + 32] = dot_nt(qt[rows], dst).astype(BF16)
        held = nxt

    go_ref[grp] += dot_nn(ot_ref[...], gy)
    gq_ref[grp] += dot_nn(dqkv_ref[...], x)
    part = dot_nn(wq_ref[grp], dqkv_ref[...])

    @pl.when(grp == 0)
    def _():
        acc_ref[...] = part

    @pl.when(grp > 0)
    def _():
        acc_ref[...] += part

    @pl.when(grp == 3)
    def _():
        gx_ref[0] = (gy.astype(F32) + acc_ref[...].T).astype(BF16)

    @pl.when(jnp.logical_and(seq == pl.num_programs(0) - 1, grp == 3))
    def _():
        for j in range(4):
            gqkv_refs[j][...] = gq_ref[j].T
            gout_refs[j][...] = go_ref[j]


def att_call(x, gy, qkvs, outs_w):
    seqs, length, width = x.shape
    group = outs_w[0].shape[0]
    heads = group // 32
    row = pl.BlockSpec((1, length, width), lambda s, j: (s, 0, 0))
    wq = pl.BlockSpec((width, 3 * group), lambda s, j: (0, 0))
    wo = pl.BlockSpec((group, width), lambda s, j: (0, 0))
    outs = pl.pallas_call(
        functools.partial(att_kernel, heads),
        grid=(seqs, 4),
        in_specs=[row, row] + [wq] * 4 + [wo] * 4,
        out_specs=[row] + [wq] * 4 + [wo] * 4,
        out_shape=[jax.ShapeDtypeStruct(x.shape, BF16)]
        + [jax.ShapeDtypeStruct((width, 3 * group), F32)] * 4
        + [jax.ShapeDtypeStruct((group, width), F32)] * 4,
        scratch_shapes=[
            pltpu.VMEM((4, width, 3 * group), BF16),
            pltpu.VMEM((4, 3 * group, width), BF16),
            pltpu.VMEM((4, group, width), BF16),
            pltpu.VMEM((3 * group, length), BF16),
            pltpu.VMEM((group, length), BF16),
            pltpu.VMEM((width, length), F32),
            pltpu.VMEM((4, 3 * group, width), F32),
            pltpu.VMEM((4, group, width), F32),
        ],
        compiler_params=pltpu.CompilerParams(
            dimension_semantics=("arbitrary", "arbitrary"), vmem_limit_bytes=60 * 1024 * 1024
        ),
        cost_estimate=pl.CostEstimate(
            flops=60 * seqs * length * width * width, bytes_accessed=40 * 1024 * 1024, transcendentals=0
        ),
        name="att_bwd",
    )(x, gy, *qkvs, *outs_w)
    return outs[0], outs[1:5], outs[5:9]


def swap(a, bit):
    return lax.ppermute(a, "tp", [(i, i ^ bit) for i in range(4)])


def gather_rel(a):
    far = swap(a, 2)
    return [a, swap(a, 1), far, swap(far, 1)]


def reduce_rel(parts, data_axes):
    own = parts[0] + swap(parts[1], 1)
    far = parts[2] + swap(parts[3], 1)
    total = own + swap(far, 2)
    for axis in data_axes:
        total = total + lax.ppermute(total, axis, [(0, 1), (1, 0)])
    return total


def solution(mesh):
    data_axes = ("dpy", "dpx")
    replicas = mesh.shape["dpy"] * mesh.shape["dpx"]
    act_spec = P(None, data_axes, None, None)
    tok_spec = P(data_axes, None, None)
    qkv_spec = P(None, None, None, "tp", None)
    wout_spec = P(None, "tp", None, None)
    up_spec = P(None, None, "tp")
    down_spec = P(None, "tp", None)

    def device_backward(x_saved, y_saved, d_out, w_qkv, w_out, w_up, w_down):
        layers, width = w_qkv.shape[0], w_qkv.shape[1]
        heads, dim = w_qkv.shape[3:]
        mine = d_out.shape[0] // 4
        start = lax.axis_index("tp") * mine
        take = lambda a: lax.dynamic_slice_in_dim(a, start, mine, axis=0)
        grad = take(d_out)
        grads = [None] * layers
        for layer in reversed(range(layers)):
            ups, downs = gather_rel(w_up[layer]), gather_rel(w_down[layer])
            qkvs = gather_rel(w_qkv[layer].reshape(width, 3 * heads * dim))
            wouts = gather_rel(w_out[layer].reshape(heads * dim, width))
            mid, gup, gdown = mlp_call(take(y_saved[layer]), grad, ups, downs)
            grad, gqkv, gout = att_call(take(x_saved[layer]), mid, qkvs, wouts)
            sums = [reduce_rel(parts, data_axes) / replicas for parts in (gqkv, gout, gup, gdown)]
            grads[layer] = (
                sums[0].reshape(width, 3, heads, dim),
                sums[1].reshape(heads, dim, width),
                sums[2],
                sums[3],
            )
        d_input = lax.all_gather(grad, "tp", axis=0, tiled=True)
        return (d_input,) + tuple(jnp.stack([g[slot] for g in grads]) for slot in range(4))

    return jax.shard_map(
        device_backward,
        mesh=mesh,
        in_specs=(act_spec, act_spec, tok_spec, qkv_spec, wout_spec, up_spec, down_spec),
        out_specs=(tok_spec, qkv_spec, wout_spec, up_spec, down_spec),
        check_vma=False,
    )
```

time: 2530 us -> 960 us (0.38)
  matrix products: 1460 us -> 0 us
  waiting for transfers between devices: 834 us -> 312 us
  Pallas kernels: 0 us -> 470 us
  other arithmetic: 199 us -> 19.6 us
  local copies, waits for them, and re-layouts: 21 us -> 91.4 us
  starting transfers between devices: 0.99 us -> 43.6 us
    dot_general x64 -> x0, matrix products: 1340 us -> none  [the longest x4 334 us: layer_backward(): jnp.einsum('bnqk,bknd->bqnd', d_scores, keys_all, preferred_element_type=...]
    psum x5 -> x0, waiting for transfers between devices: 834 us -> none  [the longest x2 502 us: layer_backward(): in_sum = lax.psum(in_part, 'tp')]
    pallas_call x0 -> x4, Pallas kernels: none -> 470 us  [the longest x2 360 us: att_call(): pl.pallas_call(functools.partial(att_kernel, heads), grid=(seqs, 4), in_s...]
    ppermute x0 -> x64, waiting for transfers between devices: none -> 312 us  [the longest x48 197 us: swap(): return lax.ppermute(a, 'tp', [(i, i ^ bit) for i in range(4)])]
    convert_element_type x8 -> x0, other arithmetic: 183 us -> none  [the longest x4 131 us: layer_backward(): probs_b = probs_f.astype(jnp.bfloat16)]
    sub x4 -> x0, matrix products: 115 us -> none  [layer_backward(): probs_f = jax.nn.softmax(scores, axis=-1)]
    slice x0 -> x4, local copies, waits for them, and re-layouts: none -> 46 us  [the longest x1 22.5 us: device_backward(): grad, gqkv, gout = att_call(take(x_saved[layer]), mid, qkvs, wouts)]
    ppermute x0 -> x64, starting transfers between devices: none -> 43.6 us  [the longest x48 23.7 us: swap(): return lax.ppermute(a, 'tp', [(i, i ^ bit) for i in range(4)])]
  transfers between devices with their start and end apart: 5 -> 65, of which waited for: 4 -> 26; matrix products, arithmetic and copies ran while one was open for 22% -> 10% of each run, Pallas kernels for 0% -> 30%
where the time goes in v1:
time: 960 us; the launch traced here: 951 us
  Pallas kernels  470 us (49%)
  waiting for transfers between devices  312 us (32%)
  local copies, waits for them, and re-layouts  91.4 us (10%)
  starting transfers between devices  43.6 us (5%)
  other arithmetic  19.6 us (2%)
  between operations  15 us (2%)
    pallas_call x2, Pallas kernels, att_call(): pl.pallas_call(functools.partial(att_kernel, heads), grid=(seqs, 4), in_s...  360 us
    ppermute x48, waiting for transfers between devices, swap(): return lax.ppermute(a, 'tp', [(i, i ^ bit) for i in range(4)])  197 us
    ppermute x16, waiting for transfers between devices, reduce_rel(): total = total + lax.ppermute(total, axis, [(0, 1), (1, 0)])  115 us
    pallas_call x2, Pallas kernels, mlp_call(): pl.pallas_call(mlp_kernel, grid=(seqs,), in_specs=[row, row] + [full] * 8...  109 us
    ppermute x48, starting transfers between devices, swap(): return lax.ppermute(a, 'tp', [(i, i ^ bit) for i in range(4)])  23.7 us
    slice x1, local copies, waits for them, and re-layouts, device_backward(): grad, gqkv, gout = att_call(take(x_saved[layer]), mid, qkvs, wouts)  22.5 us
    slice x1, local copies, waits for them, and re-layouts, device_backward(): mid, gup, gdown = mlp_call(take(y_saved[layer]), grad, ups, downs)  22.4 us
    dynamic_slice x5, local copies, waits for them, and re-layouts, device_backward(): take = lambda a: lax.dynamic_slice_in_dim(a, start, mine, axis=0)  22.2 us
  transfers between devices with their start and end apart: 65, of which 26 were waited for; matrix products, arithmetic and copies ran while one was open for 10% of the time, Pallas kernels for 30%

profile of v1, /device:TPU:0, one launch (start us, length us, event | category | flops | bytes accessed | tf_op | source)
XLA Modules:
  0.0 951.3 jit_solution(2457999727946275871)
XLA Ops:
  16.4 22.5 %fusion.1 = (bf16[1,32,512,512]{3,2,1,0:T(8,128)(2,1)}, bf16[1,32,512,512]{3,2,1,0:T(8,128)(2,1)}) fusion(bf16[2,32,512,512]{3,2,1,0:T(8,128)(2,1)} %param.7), kind=kLoop, calls=%fused_computation.30 | loop fusion | bytes 67108864 | tf_op jit(solution)/shard_map/slice | solution.py:256
  38.9 22.4 %fusion = (bf16[1,32,512,512]{3,2,1,0:T(8,128)(2,1)}, bf16[1,32,512,512]{3,2,1,0:T(8,128)(2,1)}) fusion(bf16[2,32,512,512]{3,2,1,0:T(8,128)(2,1)} %param.8), kind=kLoop, calls=%fused_computation.29 | loop fusion | bytes 67108864 | tf_op jit(solution)/shard_map/slice | solution.py:255
  90.1 54.4 %mlp_bwd.2 = (bf16[8,512,512]{2,1,0:T(8,128)(2,1)}, f32[512,512]{1,0:T(8,128)}, f32[512,512]{1,0:T(8,128)}, f32[512,512]{1,0:T(8,128)}, f32[512,512]{1,0:T(8,128...) custom-call(bf16[8,512,512]{2,1,0:T(8,128)(2,1)} %dynamic-slice_bitcast_fusion.refs_0_, ...), custom_call_target="tpu_custom_call" | custom-call | flops 42949672960 | bytes 41943040 | tf_op jit(solution)/shard_map/mlp_bwd/pallas_call | solution.py:83
  147.3 180.2 %att_bwd.2 = (bf16[8,512,512]{2,1,0:T(8,128)(2,1)}, f32[512,384]{1,0:T(8,128)}, f32[512,384]{1,0:T(8,128)}, f32[512,384]{1,0:T(8,128)}, f32[512,384]{1,0:T(8,128...) custom-call(bf16[8,512,512]{2,1,0:T(8,128)(2,1)} %dynamic-slice_bitcast_fusion.1.refs_0_, ...), custom_call_target="tpu_custom_call" | custom-call | flops 64424509440 | bytes 41943040 | tf_op jit(solution)/shard_map/att_bwd/pallas_call | solution.py:186
  328.6 55.0 %mlp_bwd.3 = (bf16[8,512,512]{2,1,0:T(8,128)(2,1)}, f32[512,512]{1,0:T(8,128)}, f32[512,512]{1,0:T(8,128)}, f32[512,512]{1,0:T(8,128)}, f32[512,512]{1,0:T(8,128...) custom-call(bf16[8,512,512]{2,1,0:T(8,128)(2,1)} %dynamic-slice_bitcast_fusion.2.refs_0_, ...), custom_call_target="tpu_custom_call" | custom-call | flops 42949672960 | bytes 41943040 | tf_op jit(solution)/shard_map/mlp_bwd/pallas_call | solution.py:83
  384.5 180.2 %att_bwd.3 = (bf16[8,512,512]{2,1,0:T(8,128)(2,1)}, f32[512,384]{1,0:T(8,128)}, f32[512,384]{1,0:T(8,128)}, f32[512,384]{1,0:T(8,128)}, f32[512,384]{1,0:T(8,128...) custom-call(bf16[8,512,512]{2,1,0:T(8,128)(2,1)} %dynamic-slice_bitcast_fusion.3.refs_0_, ...), custom_call_target="tpu_custom_call" | custom-call | flops 64424509440 | bytes 41943040 | tf_op jit(solution)/shard_map/att_bwd/pallas_call | solution.py:186
  569.8 6.3 collective-permute-done.41
  576.4 13.6 %collective-permute-done.36 = f32[128,512]{1,0:T(8,128)S(1)} collective-permute-done((f32[128,512]{1,0:T(8,128)S(1)}, f32[128,512]{1,0:T(8,128)S(1)}, u32[]{:S(2)}, u32[]{:S(2)}) %collective-permute-start.36) | collective-permute-done | bytes 262176 | tf_op jit(solution)/shard_map/ppermute | solution.py:216
  592.4 6.5 collective-permute-done.42
  602.2 4.7 collective-permute-done.37
  613.1 33.2 %collective-permute-done.31 = f32[512,384]{1,0:T(8,128)S(1)} collective-permute-done((f32[512,384]{1,0:T(8,128)S(1)}, f32[512,384]{1,0:T(8,128)S(1)}, u32[]{:S(2)}, u32[]{:S(2)}) %collective-permute-start.31) | collective-permute-done | bytes 786464 | tf_op jit(solution)/shard_map/ppermute | solution.py:216
  647.2 32.7 %collective-permute-done.26 = f32[512,384]{1,0:T(8,128)S(1)} collective-permute-done((f32[512,384]{1,0:T(8,128)S(1)}, f32[512,384]{1,0:T(8,128)S(1)}, u32[]{:S(2)}, u32[]{:S(2)}) %collective-permute-start.26) | collective-permute-done | bytes 786464 | tf_op jit(solution)/shard_map/ppermute | solution.py:216
  682.4 42.5 %collective-permute-done.51 = f32[512,512]{1,0:T(8,128)S(1)} collective-permute-done((f32[512,512]{1,0:T(8,128)S(1)}, f32[512,512]{1,0:T(8,128)S(1)}, u32[]{:S(2)}, u32[]{:S(2)}) %collective-permute-start.51) | collective-permute-done | bytes 1048608 | tf_op jit(solution)/shard_map/ppermute | solution.py:216
  727.3 25.2 %collective-permute-done.46 = f32[512,512]{1,0:T(8,128)S(1)} collective-permute-done((f32[512,512]{1,0:T(8,128)S(1)}, f32[512,512]{1,0:T(8,128)S(1)}, u32[]{:S(2)}, u32[]{:S(2)}) %collective-permute-start.46) | collective-permute-done | bytes 1048608 | tf_op jit(solution)/shard_map/ppermute | solution.py:216
  754.3 20.6 %collective-permute-done.61 = f32[512,512]{1,0:T(8,128)S(1)} collective-permute-done((f32[512,512]{1,0:T(8,128)S(1)}, f32[512,512]{1,0:T(8,128)S(1)}, u32[]{:S(2)}, u32[]{:S(2)}) %collective-permute-start.61) | collective-permute-done | bytes 1048608 | tf_op jit(solution)/shard_map/ppermute | solution.py:216
  777.5 19.6 %collective-permute-done.56 = f32[512,512]{1,0:T(8,128)S(1)} collective-permute-done((f32[512,512]{1,0:T(8,128)S(1)}, f32[512,512]{1,0:T(8,128)S(1)}, u32[]{:S(2)}, u32[]{:S(2)}) %collective-permute-start.56) | collective-permute-done | bytes 1048608 | tf_op jit(solution)/shard_map/ppermute | solution.py:216
  800.6 5.7 collective-permute-done.38
  810.5 19.1 %collective-permute-done.62 = f32[512,512]{1,0:T(8,128)S(1)} collective-permute-done((f32[512,512]{1,0:T(8,128)S(1)}, f32[512,512]{1,0:T(8,128)S(1)}, u32[]{:S(2)}, u32[]{:S(2)}) %collective-permute-start.62) | collective-permute-done | bytes 1048608 | tf_op jit(solution)/shard_map/ppermute | solution.py:229
  833.7 6.3 collective-permute-done.28
  856.1 6.4 collective-permute-done.53
  863.9 21.0 %collective-permute-done.48 = f32[512,512]{1,0:T(8,128)} collective-permute-done((f32[512,512]{1,0:T(8,128)S(1)}, f32[512,512]{1,0:T(8,128)}, u32[]{:S(2)}, u32[]{:S(2)}) %collective-permute-start.48) | collective-permute-done | bytes 1048608 | tf_op jit(solution)/shard_map/ppermute | solution.py:229
  887.9 19.5 %collective-permute-done.63 = f32[512,512]{1,0:T(8,128)} collective-permute-done((f32[512,512]{1,0:T(8,128)S(1)}, f32[512,512]{1,0:T(8,128)}, u32[]{:S(2)}, u32[]{:S(2)}) %collective-permute-start.63) | collective-permute-done | bytes 1048608 | tf_op jit(solution)/shard_map/ppermute | solution.py:229
  908.9 19.9 %collective-permute-done.58 = f32[512,512]{1,0:T(8,128)S(1)} collective-permute-done((f32[512,512]{1,0:T(8,128)S(1)}, f32[512,512]{1,0:T(8,128)S(1)}, u32[]{:S(2)}, u32[]{:S(2)}) %collective-permute-start.58) | collective-permute-done | bytes 1048608 | tf_op jit(solution)/shard_map/ppermute | solution.py:229
  930.5 13.8 %copy.33 = bf16[32,512,512]{2,1,0:T(8,128)(2,1)} copy(bf16[32,512,512]{2,1,0:T(8,128)(2,1)} %all-gather.2.cloned.1.call-done) | data formatting | bytes 33554432
  (253 shorter events, 104.9 us)
Async XLA Ops:
  7.2 923.3 %all-gather.2.cloned.1.call-start = ((), (), s32[]{:S(2)}) async-start(), calls=%async_computation | async-start | bytes 20971520 | tf_op jit(solution)/shard_map/all_gather | solution.py:264
  8.5 79.0 %collective-permute-start = (bf16[512,512]{1,0:T(8,128)(2,1)S(1)}, bf16[512,512]{1,0:T(8,128)(2,1)}, u32[]{:S(2)}, u32[]{:S(2)}) collective-permute-start(bf16[512,512]{1,0:T(8,128)(2,1)S(1)} %get-tuple-element.84.refs_2_), channel_id=1, source_target_pairs={{0,1},{1,0},{2,3},{3,2},{4,5},{5,4},{6,7},{7,6},{8,9},{9,8},{10,11... | collective-permute-start | bytes 1572872 | tf_op jit(solution)/shard_map/ppermute | solution.py:216
  9.3 61.5 %collective-permute-start.1 = (bf16[512,512]{1,0:T(8,128)(2,1)S(1)}, bf16[512,512]{1,0:T(8,128)(2,1)}, u32[]{:S(2)}, u32[]{:S(2)}) collective-permute-start(bf16[512,512]{1,0:T(8,128)(2,1)S(1)} %get-tuple-element.84.refs_2_), channel_id=1, source_target_pairs={{0,2},{1,3},{2,0},{3,1},{4,6},{5,7},{6,4},{7,5},{8,10},{9,11},{10,... | collective-permute-start | bytes 1572872 | tf_op jit(solution)/shard_map/ppermute | solution.py:216
  12.8 57.5 %collective-permute-start.9 = (bf16[128,512]{1,0:T(8,128)(2,1)S(1)}, bf16[128,512]{1,0:T(8,128)(2,1)S(1)}, u32[]{:S(2)}, u32[]{:S(2)}) collective-permute-start(bf16[128,512]{1,0:T(8,128)(2,1)S(1)} %bitcast.41), channel_id=1, source_target_pairs={{0,1},{1,0},{2,3},{3,2},{4,5},{5,4},{6,7},{7,6},{8,9},{9,8},{10,11... | collective-permute-start | bytes 393224 | tf_op jit(solution)/shard_map/ppermute | solution.py:216
  13.0 57.4 %collective-permute-start.10 = (bf16[128,512]{1,0:T(8,128)(2,1)S(1)}, bf16[128,512]{1,0:T(8,128)(2,1)S(1)}, u32[]{:S(2)}, u32[]{:S(2)}) collective-permute-start(bf16[128,512]{1,0:T(8,128)(2,1)S(1)} %bitcast.42), channel_id=1, source_target_pairs={{0,2},{1,3},{2,0},{3,1},{4,6},{5,7},{6,4},{7,5},{8,10},{9,11},{10,... | collective-permute-start | bytes 393224 | tf_op jit(solution)/shard_map/ppermute | solution.py:216
  87.5 57.1 %collective-permute-start.6 = (bf16[512,384]{1,0:T(8,128)(2,1)S(1)}, bf16[512,384]{1,0:T(8,128)(2,1)}, u32[]{:S(2)}, u32[]{:S(2)}) collective-permute-start(bf16[512,384]{1,0:T(8,128)(2,1)S(1)} %copy.26.refs_2_), channel_id=1, source_target_pairs={{0,1},{1,0},{2,3},{3,2},{4,5},{5,4},{6,7},{7,6},{8,9},{9,8},{10,11... | collective-permute-start | bytes 1179656 | tf_op jit(solution)/shard_map/ppermute | solution.py:216
  87.5 57.5 %collective-permute-start.13 = (bf16[512,512]{1,0:T(8,128)(2,1)S(1)}, bf16[512,512]{1,0:T(8,128)(2,1)S(1)}, u32[]{:S(2)}, u32[]{:S(2)}) collective-permute-start(bf16[512,512]{1,0:T(8,128)(2,1)S(1)} %get-tuple-element.83.refs_2_), channel_id=1, source_target_pairs={{0,2},{1,3},{2,0},{3,1},{4,6},{5,7},{6,4},{7,5},{8,10},{9,11},{10,... | collective-permute-start | bytes 1572872 | tf_op jit(solution)/shard_map/ppermute | solution.py:216
  89.2 57.5 %collective-permute-start.16 = (bf16[512,512]{1,0:T(8,128)(2,1)S(1)}, bf16[512,512]{1,0:T(8,128)(2,1)S(1)}, u32[]{:S(2)}, u32[]{:S(2)}) collective-permute-start(bf16[512,512]{1,0:T(8,128)(2,1)S(1)} %get-tuple-element.81.refs_6_), channel_id=1, source_target_pairs={{0,2},{1,3},{2,0},{3,1},{4,6},{5,7},{6,4},{7,5},{8,10},{9,11},{10,... | collective-permute-start | bytes 1572872 | tf_op jit(solution)/shard_map/ppermute | solution.py:216
  89.6 57.2 %collective-permute-start.8 = (bf16[512,384]{1,0:T(8,128)(2,1)S(1)}, bf16[512,384]{1,0:T(8,128)(2,1)}, u32[]{:S(2)}, u32[]{:S(2)}) collective-permute-start(bf16[512,384]{1,0:T(8,128)(2,1)S(1)} %collective-permute-done.7.refs_4_), channel_id=1, source_target_pairs={{0,1},{1,0},{2,3},{3,2},{4,5},{5,4},{6,7},{7,6},{8,9},{9,8},{10,11... | collective-permute-start | bytes 1179656 | tf_op jit(solution)/shard_map/ppermute | solution.py:216
  144.5 183.1 %collective-permute-start.12 = (bf16[512,512]{1,0:T(8,128)(2,1)S(1)}, bf16[512,512]{1,0:T(8,128)(2,1)S(1)}, u32[]{:S(2)}, u32[]{:S(2)}) collective-permute-start(bf16[512,512]{1,0:T(8,128)(2,1)S(1)} %get-tuple-element.83.refs_2_), channel_id=1, source_target_pairs={{0,1},{1,0},{2,3},{3,2},{4,5},{5,4},{6,7},{7,6},{8,9},{9,8},{10,11... | collective-permute-start | bytes 1572872 | tf_op jit(solution)/shard_map/ppermute | solution.py:216
  144.6 183.5 %collective-permute-start.15 = (bf16[512,512]{1,0:T(8,128)(2,1)S(1)}, bf16[512,512]{1,0:T(8,128)(2,1)}, u32[]{:S(2)}, u32[]{:S(2)}) collective-permute-start(bf16[512,512]{1,0:T(8,128)(2,1)S(1)} %get-tuple-element.81.refs_6_), channel_id=1, source_target_pairs={{0,1},{1,0},{2,3},{3,2},{4,5},{5,4},{6,7},{7,6},{8,9},{9,8},{10,11... | collective-permute-start | bytes 1572872 | tf_op jit(solution)/shard_map/ppermute | solution.py:216
  145.0 182.4 %collective-permute-start.19 = (bf16[512,384]{1,0:T(8,128)(2,1)S(1)}, bf16[512,384]{1,0:T(8,128)(2,1)S(1)}, u32[]{:S(2)}, u32[]{:S(2)}) collective-permute-start(bf16[512,384]{1,0:T(8,128)(2,1)S(1)} %copy.29.refs_2_), channel_id=1, source_target_pairs={{0,2},{1,3},{2,0},{3,1},{4,6},{5,7},{6,4},{7,5},{8,10},{9,11},{10,... | collective-permute-start | bytes 1179656 | tf_op jit(solution)/shard_map/ppermute | solution.py:216
  146.7 181.4 %collective-permute-start.14 = (bf16[512,512]{1,0:T(8,128)(2,1)S(1)}, bf16[512,512]{1,0:T(8,128)(2,1)}, u32[]{:S(2)}, u32[]{:S(2)}) collective-permute-start(bf16[512,512]{1,0:T(8,128)(2,1)S(1)} %collective-permute-done.13.refs_4_), channel_id=1, source_target_pairs={{0,1},{1,0},{2,3},{3,2},{4,5},{5,4},{6,7},{7,6},{8,9},{9,8},{10,11... | collective-permute-start | bytes 1572872 | tf_op jit(solution)/shard_map/ppermute | solution.py:216
  146.8 181.8 %collective-permute-start.17 = (bf16[512,512]{1,0:T(8,128)(2,1)S(1)}, bf16[512,512]{1,0:T(8,128)(2,1)}, u32[]{:S(2)}, u32[]{:S(2)}) collective-permute-start(bf16[512,512]{1,0:T(8,128)(2,1)S(1)} %collective-permute-done.16.refs_8_), channel_id=1, source_target_pairs={{0,1},{1,0},{2,3},{3,2},{4,5},{5,4},{6,7},{7,6},{8,9},{9,8},{10,11... | collective-permute-start | bytes 1572872 | tf_op jit(solution)/shard_map/ppermute | solution.py:216
  609.6 70.4 %collective-permute-start.26 = (f32[512,384]{1,0:T(8,128)S(1)}, f32[512,384]{1,0:T(8,128)S(1)}, u32[]{:S(2)}, u32[]{:S(2)}) collective-permute-start(f32[512,384]{1,0:T(8,128)S(1)} %add.129), channel_id=1, source_target_pairs={{0,2},{1,3},{2,0},{3,1},{4,6},{5,7},{6,4},{7,5},{8,10},{9,11},{10,... | collective-permute-start | bytes 2359304 | tf_op jit(solution)/shard_map/ppermute | solution.py:216
  611.4 69.4 %collective-permute-start.59 = (f32[512,512]{1,0:T(8,128)S(1)}, f32[512,512]{1,0:T(8,128)S(1)}, u32[]{:S(2)}, u32[]{:S(2)}) collective-permute-start(f32[512,512]{1,0:T(8,128)S(1)} %copy-done.25), channel_id=1, source_target_pairs={{0,1},{1,0},{2,3},{3,2},{4,5},{5,4},{6,7},{7,6},{8,9},{9,8},{10,11... | collective-permute-start | bytes 3145736 | tf_op jit(solution)/shard_map/ppermute | solution.py:216
  611.4 113.5 %collective-permute-start.51 = (f32[512,512]{1,0:T(8,128)S(1)}, f32[512,512]{1,0:T(8,128)S(1)}, u32[]{:S(2)}, u32[]{:S(2)}) collective-permute-start(f32[512,512]{1,0:T(8,128)S(1)} %add.154), channel_id=1, source_target_pairs={{0,2},{1,3},{2,0},{3,1},{4,6},{5,7},{6,4},{7,5},{8,10},{9,11},{10,... | collective-permute-start | bytes 3145736 | tf_op jit(solution)/shard_map/ppermute | solution.py:216
  612.7 112.9 %collective-permute-start.54 = (f32[512,512]{1,0:T(8,128)S(1)}, f32[512,512]{1,0:T(8,128)S(1)}, u32[]{:S(2)}, u32[]{:S(2)}) collective-permute-start(f32[512,512]{1,0:T(8,128)S(1)} %copy-done.27), channel_id=1, source_target_pairs={{0,1},{1,0},{2,3},{3,2},{4,5},{5,4},{6,7},{7,6},{8,9},{9,8},{10,11... | collective-permute-start | bytes 3145736 | tf_op jit(solution)/shard_map/ppermute | solution.py:216
  646.3 106.2 %collective-permute-start.46 = (f32[512,512]{1,0:T(8,128)S(1)}, f32[512,512]{1,0:T(8,128)S(1)}, u32[]{:S(2)}, u32[]{:S(2)}) collective-permute-start(f32[512,512]{1,0:T(8,128)S(1)} %add.149), channel_id=1, source_target_pairs={{0,2},{1,3},{2,0},{3,1},{4,6},{5,7},{6,4},{7,5},{8,10},{9,11},{10,... | collective-permute-start | bytes 3145736 | tf_op jit(solution)/shard_map/ppermute | solution.py:216
  680.0 95.0 %collective-permute-start.61 = (f32[512,512]{1,0:T(8,128)S(1)}, f32[512,512]{1,0:T(8,128)S(1)}, u32[]{:S(2)}, u32[]{:S(2)}) collective-permute-start(f32[512,512]{1,0:T(8,128)S(1)} %add.164), channel_id=1, source_target_pairs={{0,2},{1,3},{2,0},{3,1},{4,6},{5,7},{6,4},{7,5},{8,10},{9,11},{10,... | collective-permute-start | bytes 3145736 | tf_op jit(solution)/shard_map/ppermute | solution.py:216
  680.8 116.3 %collective-permute-start.56 = (f32[512,512]{1,0:T(8,128)S(1)}, f32[512,512]{1,0:T(8,128)S(1)}, u32[]{:S(2)}, u32[]{:S(2)}) collective-permute-start(f32[512,512]{1,0:T(8,128)S(1)} %add.159), channel_id=1, source_target_pairs={{0,2},{1,3},{2,0},{3,1},{4,6},{5,7},{6,4},{7,5},{8,10},{9,11},{10,... | collective-permute-start | bytes 3145736 | tf_op jit(solution)/shard_map/ppermute | solution.py:216
  725.6 73.0 %collective-permute-start.27 = (f32[512,384]{1,0:T(8,128)S(1)}, f32[512,384]{1,0:T(8,128)S(1)}, u32[]{:S(2)}, u32[]{:S(2)}) collective-permute-start(f32[512,384]{1,0:T(8,128)S(1)} %add_add_fusion.5), channel_id=1, source_target_pairs={{0,8},{8,0},{1,9},{9,1},{2,10},{10,2},{3,11},{11,3},{4,12},{12,4},... | collective-permute-start | bytes 2359304 | tf_op jit(solution)/shard_map/ppermute | solution.py:229
  832.2 75.2 %collective-permute-start.63 = (f32[512,512]{1,0:T(8,128)S(1)}, f32[512,512]{1,0:T(8,128)}, u32[]{:S(2)}, u32[]{:S(2)}) collective-permute-start(f32[512,512]{1,0:T(8,128)S(1)} %add.166), channel_id=1, source_target_pairs={{0,4},{4,0},{1,5},{5,1},{2,6},{6,2},{3,7},{7,3},{8,12},{12,8},{9,1... | collective-permute-start | bytes 3145736 | tf_op jit(solution)/shard_map/ppermute | solution.py:229
  851.8 76.9 %collective-permute-start.58 = (f32[512,512]{1,0:T(8,128)S(1)}, f32[512,512]{1,0:T(8,128)S(1)}, u32[]{:S(2)}, u32[]{:S(2)}) collective-permute-start(f32[512,512]{1,0:T(8,128)S(1)} %add.161), channel_id=1, source_target_pairs={{0,4},{4,0},{1,5},{5,1},{2,6},{6,2},{3,7},{7,3},{8,12},{12,8},{9,1... | collective-permute-start | bytes 3145736 | tf_op jit(solution)/shard_map/ppermute | solution.py:229
  (86 other events, 3585.5 us)
Sparse Core Ops, SparseCore 0:
  565.0 172.4 all-gather.1

commit v2 on v1

v2 whole, which is shorter than its diff:
```python
import functools

import jax
import jax.numpy as jnp
from jax import lax
from jax.experimental import pallas as pl
from jax.experimental.pallas import tpu as pltpu
from jax.sharding import PartitionSpec as P

F32 = jnp.float32
BF16 = jnp.bfloat16
MESH = pl.DeviceIdType.MESH
LOG2E = 1.4426950408889634
GELU_C = 0.7978845608028654
GELU_K = 0.044715
TP = 4
DIM = 32
VMEM_LIMIT = 60 * 1024 * 1024


def dot_nn(a, b):
    return lax.dot_general(a, b, (((1,), (0,)), ((), ())), preferred_element_type=F32)


def dot_nt(a, b):
    return lax.dot_general(a, b, (((1,), (1,)), ((), ())), preferred_element_type=F32)


def first_row(seqs):
    return lax.axis_index("tp") * seqs


def gelu_pair(h, da):
    h2 = h * h
    th = jnp.tanh(h * (GELU_C + (GELU_C * GELU_K) * h2))
    q = 0.5 + 0.5 * th
    act = h * q
    slope = (2.0 * GELU_C) + (6.0 * GELU_C * GELU_K) * h2
    dh = da * (q + act * ((1.0 - q) * slope))
    return act.astype(BF16), dh.astype(BF16)


def mlp_kernel(y_ref, g_ref, w_ref, gy_ref, gw_ref, upt_ref, yt_ref, dht_ref, acc_ref):
    step = pl.program_id(0)
    width = y_ref.shape[-1]

    @pl.when(step == 0)
    def _():
        for j in range(TP):
            upt_ref[j] = w_ref[j, 0:width].T
        gw_ref[...] = jnp.zeros_like(gw_ref)

    y = y_ref[...]
    g = g_ref[...]
    yt_ref[...] = y.T
    sub = 256
    blocks = [(j, k) for j in range(TP) for k in range(width // sub)]

    def first(j, k):
        rows = slice(k * sub, (k + 1) * sub)
        return dot_nt(upt_ref[j, rows, :], y), dot_nt(w_ref[j, width + k * sub : width + (k + 1) * sub], g)

    held = first(*blocks[0])
    for i, (j, k) in enumerate(blocks):
        rows = slice(k * sub, (k + 1) * sub)
        nxt = first(*blocks[i + 1]) if i + 1 < len(blocks) else None
        at, dht = gelu_pair(*held)
        dht_ref[j, rows, :] = dht
        gw_ref[j, width + k * sub : width + (k + 1) * sub] += dot_nn(at, g)
        gw_ref[j, 0:width, rows] += dot_nt(yt_ref[...], dht)
        if k == 1:
            part = dot_nn(w_ref[j, 0:width], dht_ref[j])
            if j == 0:
                acc_ref[...] = part
            else:
                acc_ref[...] += part
        held = nxt
    gy_ref[...] = (g.astype(F32) + acc_ref[...].T).astype(BF16)


def mlp_call(y_saved, layer, g, g_is_part, w):
    length, width = y_saved.shape[2:]
    seqs = y_saved.shape[1] // TP
    g_map = (lambda s: (s, 0, 0)) if g_is_part else (lambda s: (first_row(seqs) + s, 0, 0))
    return pl.pallas_call(
        mlp_kernel,
        grid_spec=pltpu.PrefetchScalarGridSpec(
            num_scalar_prefetch=0,
            grid=(seqs,),
            in_specs=[
                pl.BlockSpec((None, None, length, width), lambda s: (layer, first_row(seqs) + s, 0, 0)),
                pl.BlockSpec((None, length, width), g_map),
                pl.BlockSpec(w.shape, lambda s: (0, 0, 0)),
            ],
            out_specs=[
                pl.BlockSpec((None, length, width), lambda s: (s, 0, 0)),
                pl.BlockSpec(w.shape, lambda s: (0, 0, 0)),
            ],
            scratch_shapes=[
                pltpu.VMEM((TP, width, width), BF16),
                pltpu.VMEM((width, length), BF16),
                pltpu.VMEM((TP, width, length), BF16),
                pltpu.VMEM((width, length), F32),
            ],
        ),
        out_shape=[jax.ShapeDtypeStruct((seqs, length, width), BF16), jax.ShapeDtypeStruct(w.shape, F32)],
        compiler_params=pltpu.CompilerParams(dimension_semantics=("arbitrary",), vmem_limit_bytes=VMEM_LIMIT),
        cost_estimate=pl.CostEstimate(
            flops=10 * seqs * length * width * 4 * width, bytes_accessed=40 * 1024 * 1024, transcendentals=0
        ),
        name="mlp_bwd",
    )(y_saved, g, w)


def att_math(grp, x, gy, w_ref, wq_ref, gw_ref, dqkv_ref, ot_ref, acc_ref):
    group = wq_ref.shape[2] // 3
    heads = group // DIM
    qkvt = dot_nt(w_ref[grp, 0 : 3 * group], x).astype(BF16)
    dot_ = dot_nt(w_ref[grp, 3 * group :], gy).astype(BF16)
    qt, kt, vt = qkvt[0:group], qkvt[group : 2 * group], qkvt[2 * group :]
    keys, values = kt.T, vt.T
    scale = DIM ** -0.5
    head_of = lax.broadcasted_iota(jnp.int32, qt.shape, 0) // DIM

    def scores(n):
        own = head_of == n
        zero = jnp.zeros_like(qt)
        return dot_nn(keys, jnp.where(own, qt, zero)), dot_nn(values, jnp.where(own, dot_, zero))

    held = scores(0)
    for n in range(heads):
        rows = slice(DIM * n, DIM * (n + 1))
        nxt = scores(n + 1) if n + 1 < heads else None
        st, dpt = held
        top = jnp.max(st, axis=0, keepdims=True)
        e = jnp.exp2((st - top) * (scale * LOG2E))
        inv = 1.0 / jnp.sum(e, axis=0, keepdims=True)
        delta = jnp.sum(e * dpt, axis=0, keepdims=True) * inv
        pt = (e * inv).astype(BF16)
        dst = ((e * (inv * scale)) * (dpt - delta)).astype(BF16)
        ot_ref[rows] = dot_nn(vt[rows], pt).astype(BF16)
        dqkv_ref[2 * group + DIM * n : 2 * group + DIM * (n + 1)] = dot_nt(dot_[rows], pt).astype(BF16)
        dqkv_ref[rows] = dot_nn(kt[rows], dst).astype(BF16)
        dqkv_ref[group + DIM * n : group + DIM * (n + 1)] = dot_nt(qt[rows], dst).astype(BF16)
        held = nxt

    gw_ref[grp, 3 * group :] += dot_nn(ot_ref[...], gy)
    gw_ref[grp, 0 : 3 * group] += dot_nn(dqkv_ref[...], x)
    part = dot_nn(wq_ref[grp], dqkv_ref[...])

    @pl.when(grp == 0)
    def _():
        acc_ref[...] = part

    @pl.when(grp > 0)
    def _():
        acc_ref[...] += part


def att_setup(w_ref, wq_ref, gw_ref):
    for j in range(TP):
        wq_ref[j] = w_ref[j, 0 : wq_ref.shape[2]].T
    gw_ref[...] = jnp.zeros_like(gw_ref)


def att_kernel(x_ref, gy_ref, w_ref, gx_ref, gw_ref, wq_ref, dqkv_ref, ot_ref, acc_ref):
    seq, grp = pl.program_id(0), pl.program_id(1)

    @pl.when(jnp.logical_and(seq == 0, grp == 0))
    def _():
        att_setup(w_ref, wq_ref, gw_ref)

    gy = gy_ref[...]
    att_math(grp, x_ref[...], gy, w_ref, wq_ref, gw_ref, dqkv_ref, ot_ref, acc_ref)

    @pl.when(grp == TP - 1)
    def _():
        gx_ref[...] = (gy.astype(F32) + acc_ref[...].T).astype(BF16)


def att_share_kernel(
    x_ref, gy_ref, w_ref, full_ref, gw_ref,
    wq_ref, dqkv_ref, ot_ref, acc_ref, gxb_ref, own_sem, send_sem, recv_sem,
):
    seq, grp = pl.program_id(0), pl.program_id(1)
    seqs = pl.num_programs(0)
    me = lax.axis_index("tp")
    near = me + 1 - 2 * (me % 2)
    far = (me + 2) % TP

    def keep(s):
        return pltpu.make_async_copy(gxb_ref.at[s % 2], full_ref.at[me * seqs + s], own_sem.at[s % 2])

    def send(kind, s):
        row = (far if kind == 2 else me) * seqs + s
        return pltpu.make_async_remote_copy(
            full_ref.at[row], full_ref.at[row], send_sem.at[kind, s], recv_sem.at[kind, s],
            device_id={"tp": far if kind == 1 else near}, device_id_type=MESH,
        )

    def arrived(kind, s):
        owner = (near, far, (near + 2) % TP)[kind]
        row = owner * seqs + s
        return pltpu.make_async_remote_copy(
            full_ref.at[row], full_ref.at[row], send_sem.at[kind, s], recv_sem.at[kind, s],
            device_id={"tp": far if kind == 1 else near}, device_id_type=MESH,
        )

    @pl.when(jnp.logical_and(seq == 0, grp == 0))
    def _():
        barrier = pltpu.get_barrier_semaphore()
        for peer in (near, far):
            pl.semaphore_signal(barrier, inc=1, device_id={"tp": peer}, device_id_type=MESH)
        pl.semaphore_wait(barrier, 2)
        att_setup(w_ref, wq_ref, gw_ref)

    @pl.when(jnp.logical_and(seq > 0, grp == 0))
    def _():
        keep(seq - 1).wait()
        send(0, seq - 1).start()
        send(1, seq - 1).start()

    @pl.when(jnp.logical_and(seq > 0, grp == 2))
    def _():
        arrived(1, seq - 1).wait_recv()
        send(2, seq - 1).start()

    gy = gy_ref[...]
    att_math(grp, x_ref[...], gy, w_ref, wq_ref, gw_ref, dqkv_ref, ot_ref, acc_ref)

    @pl.when(grp == TP - 1)
    def _():
        gxb_ref[seq % 2] = (gy.astype(F32) + acc_ref[...].T).astype(BF16)
        keep(seq).start()

    @pl.when(jnp.logical_and(seq == seqs - 1, grp == TP - 1))
    def _():
        keep(seq).wait()
        send(0, seq).start()
        send(1, seq).start()
        arrived(1, seq).wait_recv()
        send(2, seq).start()

        @pl.loop(0, seqs)
        def _(s):
            for kind in range(3):
                send(kind, s).wait_send()
            arrived(0, s).wait_recv()
            arrived(2, s).wait_recv()


def att_call(x_saved, layer, gy, w, share):
    length, width = x_saved.shape[2:]
    seqs = x_saved.shape[1] // TP
    group = w.shape[1] // 4
    scratch = [
        pltpu.VMEM((TP, width, 3 * group), BF16),
        pltpu.VMEM((3 * group, length), BF16),
        pltpu.VMEM((group, length), BF16),
        pltpu.VMEM((width, length), F32),
    ]
    row = pl.BlockSpec((None, length, width), lambda s, j: (s, 0, 0))
    whole = pl.BlockSpec(w.shape, lambda s, j: (0, 0, 0))
    if share:
        scratch += [
            pltpu.VMEM((2, length, width), BF16),
            pltpu.SemaphoreType.DMA((2,)),
            pltpu.SemaphoreType.DMA((3, seqs)),
            pltpu.SemaphoreType.DMA((3, seqs)),
        ]
        gx_shape = jax.ShapeDtypeStruct(x_saved.shape[1:], BF16)
        gx_spec = pl.BlockSpec(memory_space=pl.ANY)
    else:
        gx_shape = jax.ShapeDtypeStruct((seqs, length, width), BF16)
        gx_spec = row
    return pl.pallas_call(
        att_share_kernel if share else att_kernel,
        grid_spec=pltpu.PrefetchScalarGridSpec(
            num_scalar_prefetch=0,
            grid=(seqs, TP),
            in_specs=[
                pl.BlockSpec((None, None, length, width), lambda s, j: (layer, first_row(seqs) + s, 0, 0)),
                row,
                whole,
            ],
            out_specs=[gx_spec, whole],
            scratch_shapes=scratch,
        ),
        out_shape=[gx_shape, jax.ShapeDtypeStruct(w.shape, F32)],
        compiler_params=pltpu.CompilerParams(
            dimension_semantics=("arbitrary", "arbitrary"),
            vmem_limit_bytes=VMEM_LIMIT,
            **({"collective_id": 0, "has_side_effects": True} if share else {}),
        ),
        cost_estimate=pl.CostEstimate(
            flops=60 * seqs * length * width * width, bytes_accessed=40 * 1024 * 1024, transcendentals=0
        ),
        name="att_bwd_share" if share else "att_bwd",
    )(x_saved, gy, w)


def solution(mesh):
    data_axes = ("dpy", "dpx")
    replicas = mesh.shape["dpy"] * mesh.shape["dpx"]
    act_spec = P(None, data_axes, None, None)
    tok_spec = P(data_axes, None, None)
    qkv_spec = P(None, None, None, "tp", None)
    wout_spec = P(None, "tp", None, None)
    up_spec = P(None, None, "tp")
    down_spec = P(None, "tp", None)

    def device_backward(x_saved, y_saved, d_out, w_qkv, w_out, w_up, w_down):
        layers, width, _, heads, dim = w_qkv.shape
        group = heads * dim
        w_qkvt = w_qkv.transpose(0, 2, 3, 4, 1).reshape(layers, 3 * group, width)
        gather = lambda *parts: lax.all_gather(jnp.concatenate(parts, axis=0), "tp", axis=0, tiled=False)
        mlp_w, att_w = [None] * layers, [None] * layers
        for layer in reversed(range(layers)):
            mlp_w[layer] = gather(w_up[layer], w_down[layer])
            att_w[layer] = gather(w_qkvt[layer], w_out[layer].reshape(group, width))

        def total(parts):
            mine = lax.psum_scatter(parts, "tp", scatter_dimension=0, tiled=False)
            return lax.psum(mine, data_axes) / replicas

        mlp_g, att_g = [None] * layers, [None] * layers
        grad = d_out
        for layer in reversed(range(layers)):
            mid, mlp_g[layer] = mlp_call(y_saved, layer, grad, layer < layers - 1, mlp_w[layer])
            grad, att_g[layer] = att_call(x_saved, layer, mid, att_w[layer], layer == 0)
        mlp_g, att_g = [total(g) for g in mlp_g], [total(g) for g in att_g]
        g_qkvt = jnp.stack([g[: 3 * group] for g in att_g]).reshape(layers, 3, heads, dim, width)
        return (
            grad,
            g_qkvt.transpose(0, 4, 1, 2, 3),
            jnp.stack([g[3 * group :] for g in att_g]).reshape(layers, heads, dim, width),
            jnp.stack([g[:width] for g in mlp_g]),
            jnp.stack([g[width:] for g in mlp_g]),
        )

    return jax.shard_map(
        device_backward,
        mesh=mesh,
        in_specs=(act_spec, act_spec, tok_spec, qkv_spec, wout_spec, up_spec, down_spec),
        out_specs=(tok_spec, qkv_spec, wout_spec, up_spec, down_spec),
        check_vma=False,
    )
```

time: 960 us -> 883 us (0.920)
  local copies, waits for them, and re-layouts: 91.4 us -> 14.7 us
  starting transfers between devices: 43.6 us -> 0.37 us
  waiting for transfers between devices: 312 us -> 346 us
  Pallas kernels: 470 us -> 497 us
    ppermute x64 -> x0, waiting for transfers between devices: 312 us -> none  [the longest x48 197 us: swap(): return lax.ppermute(a, 'tp', [(i, i ^ bit) for i in range(4)])]
    reduce_scatter x0 -> x4, waiting for transfers between devices: none -> 178 us  [total(): mine = lax.psum_scatter(parts, 'tp', scatter_dimension=0, tiled=False)]
    psum x0 -> x1, waiting for transfers between devices: none -> 134 us  [total(): return lax.psum(mine, data_axes) / replicas]
    slice x4 -> x10, local copies, waits for them, and re-layouts: 46 us -> 1.71 us  [the longest x4 1.31 us: device_backward(): g[:3 * group]]
    ppermute x64 -> x0, starting transfers between devices: 43.6 us -> none  [the longest x48 23.7 us: swap(): return lax.ppermute(a, 'tp', [(i, i ^ bit) for i in range(4)])]
    all_gather x1 -> x4, waiting for transfers between devices: 0.01 us -> 31.9 us  [device_backward(): lax.all_gather(jnp.concatenate(parts, axis=0), 'tp', axis=0, tiled=False)]
    pallas_call x4, Pallas kernels: 470 us -> 497 us  [the longest x2 385 us: att_call(): pl.pallas_call(att_share_kernel if share else att_kernel, grid_spec=pltpu...]
    dynamic_slice x5 -> x0, local copies, waits for them, and re-layouts: 22.2 us -> none  [device_backward(): take = lambda a: lax.dynamic_slice_in_dim(a, start, mine, axis=0)]
  transfers between devices with their start and end apart: 65 -> 9, of which waited for: 26 -> 5; matrix products, arithmetic and copies ran while one was open for 10% -> 0% of each run, Pallas kernels for 30% -> 56%
where the time goes in v2:
time: 883 us
  Pallas kernels  497 us (56%)
  waiting for transfers between devices  346 us (39%)
  local copies, waits for them, and re-layouts  14.7 us (2%)
  between operations  14 us (2%)
  other arithmetic  10.8 us (1%)
    pallas_call x2, Pallas kernels, att_call(): pl.pallas_call(att_share_kernel if share else att_kernel, grid_spec=pltpu...  385 us
    reduce_scatter x4, waiting for transfers between devices, total(): mine = lax.psum_scatter(parts, 'tp', scatter_dimension=0, tiled=False)  178 us
    psum x1, waiting for transfers between devices, total(): return lax.psum(mine, data_axes) / replicas  134 us
    pallas_call x2, Pallas kernels, mlp_call(): pl.pallas_call(mlp_kernel, grid_spec=pltpu.PrefetchScalarGridSpec(num_sca...  112 us
    all_gather x4, waiting for transfers between devices, device_backward(): lax.all_gather(jnp.concatenate(parts, axis=0), 'tp', axis=0, tiled=False)  31.9 us
  transfers between devices with their start and end apart: 9, of which 5 were waited for; matrix products, arithmetic and copies ran while one was open for 0% of the time, Pallas kernels for 56%

profile of v2, /device:TPU:0, one launch (start us, length us, event | category | flops | bytes accessed | tf_op | source)
XLA Modules:
  0.0 882.9 jit_solution(16886001607700791529)
XLA Ops:
  7.2 1.7 slice_bitcast_fusion.4
  8.9 1.0 pad_maximum_fusion.2
  10.5 0.8 pad_maximum_fusion.4
  11.4 1.0 pad_maximum_fusion.3
  12.6 0.8 pad_maximum_fusion.5
  13.5 31.9 %all-gather.9.cloned.1.call-done = bf16[4096,512]{1,0:T(8,128)(2,1)} async-done(((bf16[1024,512]{1,0:T(8,128)(2,1)}), bf16[4096,512]{1,0:T(8,128)(2,1)}) %all-gather.9.cloned.1.call-update) | async-done | bytes 4194320 | tf_op jit(solution)/shard_map/all_gather | solution.py:316
  45.4 56.2 %mlp_bwd.2 = (bf16[8,512,512]{2,1,0:T(8,128)(2,1)}, f32[4,1024,512]{2,1,0:T(8,128)}) custom-call(bf16[2,32,512,512]{3,2,1,0:T(8,128)(2,1)} %y_ref.3, bf16[32,512,512]{2,1,0:T(8,128)(2,1)} %g_ref.1, bf16[4,1024,512]{2,1,0:T(8,128)(2,1)} %bitcast.50), custom_call_target="tpu_custom_call" | custom-call | flops 42949672960 | bytes 41943040 | tf_op jit(solution)/shard_map/mlp_bwd/pallas_call | solution.py:85
  101.6 178.4 %att_bwd.1 = (bf16[8,512,512]{2,1,0:T(8,128)(2,1)}, f32[4,512,512]{2,1,0:T(8,128)}) custom-call(bf16[2,32,512,512]{3,2,1,0:T(8,128)(2,1)} %x_ref.3, bf16[8,512,512]{2,1,0:T(8,128)(2,1)} %get-tuple-element.13.gy_ref, bf16[4,512,512]{2,1,0:T(8,128)(2,1)} %bitcast.52), custom_call_target="tpu_custom_call" | custom-call | flops 64424509440 | bytes 41943040 | tf_op jit(solution)/shard_map/att_bwd/pallas_call | solution.py:276
  280.0 56.3 %mlp_bwd.3 = (bf16[8,512,512]{2,1,0:T(8,128)(2,1)}, f32[4,1024,512]{2,1,0:T(8,128)}) custom-call(bf16[2,32,512,512]{3,2,1,0:T(8,128)(2,1)} %y_ref.3, bf16[8,512,512]{2,1,0:T(8,128)(2,1)} %get-tuple-element.14.g_ref, bf16[4,1024,512]{2,1,0:T(8,128)(2,1)} %bitcast.51), custom_call_target="tpu_custom_call" | custom-call | flops 42949672960 | bytes 41943040 | tf_op jit(solution)/shard_map/mlp_bwd/pallas_call | solution.py:85
  336.3 206.3 %att_bwd_share.1 = (bf16[32,512,512]{2,1,0:T(8,128)(2,1)}, f32[4,512,512]{2,1,0:T(8,128)}) custom-call(bf16[2,32,512,512]{3,2,1,0:T(8,128)(2,1)} %x_ref.3, bf16[8,512,512]{2,1,0:T(8,128)(2,1)} %get-tuple-element.15.gy_ref, bf16[4,512,512]{2,1,0:T(8,128)(2,1)} %bitcast.53), custom_call_target="tpu_custom_call" | custom-call | flops 64424509440 | bytes 41943040 | tf_op jit(solution)/shard_map/att_bwd_share/pallas_call | solution.py:276
  544.2 38.6 %reduce-scatter.5.cloned.1.call-done = f32[1,512,512]{2,1,0:T(8,128)} async-done(((f32[4,512,512]{2,1,0:T(8,128)}), f32[1,512,512]{2,1,0:T(8,128)}) %reduce-scatter.5.cloned.1.call-update) | async-done | bytes 1048592 | tf_op jit(solution)/shard_map/reduce_scatter | solution.py:323
  582.8 70.1 %reduce-scatter.11.cloned.1.call-done = f32[1,1024,512]{2,1,0:T(8,128)} async-done(((f32[4,1024,512]{2,1,0:T(8,128)}), f32[1,1024,512]{2,1,0:T(8,128)}) %reduce-scatter.11.cloned.1.call-update) | async-done | bytes 2097168 | tf_op jit(solution)/shard_map/reduce_scatter | solution.py:323
  652.9 69.5 %reduce-scatter.9.cloned.1.call-done = f32[1,1024,512]{2,1,0:T(8,128)} async-done(((f32[4,1024,512]{2,1,0:T(8,128)}), f32[1,1024,512]{2,1,0:T(8,128)}) %reduce-scatter.9.cloned.1.call-update) | async-done | bytes 2097168 | tf_op jit(solution)/shard_map/reduce_scatter | solution.py:323
  722.5 134.2 %all-reduce.3.cloned.1.call-done = (f32[512,512]{1,0:T(8,128)}, f32[512,512]{1,0:T(8,128)}, f32[1024,512]{1,0:T(8,128)}, f32[1024,512]{1,0:T(8,128)}) async-done(((f32[512,512]{1,0:T(8,128)}, f32[512,512]{1,0:T(8,128)}, f32[1024,512]{1,0:T(8,128)}, f32[1024,512]{1,0:T(8,128)}), (f32[512,512]{1,0:T(8,128)}, f32[512,512]{1,0:T(8,128)}, f32[1024,512]{1,0:T(8,128)}, ...) | async-done | bytes 6291472 | tf_op jit(solution)/shard_map/psum | solution.py:324
  856.6 1.4 broadcast_multiply_fusion.2
  858.3 0.7 copy-done
  859.0 1.1 copy-done.3
  860.6 1.7 copy-done.2
  862.7 1.1 slice-done.5
  864.0 1.3 maximum_bitcast_fusion
  865.6 0.8 pad_maximum_fusion.6
  866.5 1.5 pad_maximum_fusion.1
  867.9 1.5 pad_maximum_fusion
  870.2 6.2 copy.17
  (56 shorter events, 4.7 us)
Async XLA Ops:
  7.2 38.2 %all-gather.9.cloned.1.call-start = ((), (), s32[]{:S(2)}) async-start(), calls=%async_computation.8 | async-start | bytes 5242880 | tf_op jit(solution)/shard_map/all_gather | solution.py:316
  8.9 1.1 copy-start.6
  8.9 1.6 copy-start.5
  10.0 91.6 %all-gather.11.cloned.1.call-start = ((), (), s32[]{:S(2)}) async-start(), calls=%async_computation.9 | async-start | bytes 2621440 | tf_op jit(solution)/shard_map/all_gather | solution.py:316
  11.4 268.6 %all-gather.13.cloned.1.call-start = ((), (), s32[]{:S(2)}) async-start(), calls=%async_computation.10 | async-start | bytes 5242880 | tf_op jit(solution)/shard_map/all_gather | solution.py:316
  12.5 323.8 %all-gather.15.cloned.1.call-start = ((), (), s32[]{:S(2)}) async-start(), calls=%async_computation.11 | async-start | bytes 2621440 | tf_op jit(solution)/shard_map/all_gather | solution.py:316
  13.4 530.8 %reduce-scatter.7.cloned.1.call-start = ((), (), s32[]{:S(2)}) async-start(), calls=%async_computation.5 | async-start | bytes 5242880 | tf_op jit(solution)/shard_map/reduce_scatter | solution.py:323
  280.0 302.9 %reduce-scatter.5.cloned.1.call-start = ((), (), s32[]{:S(2)}) async-start(), calls=%async_computation.4 | async-start | bytes 5242880 | tf_op jit(solution)/shard_map/reduce_scatter | solution.py:323
  542.7 110.3 %reduce-scatter.11.cloned.1.call-start = ((), (), s32[]{:S(2)}) async-start(), calls=%async_computation.7 | async-start | bytes 10485760 | tf_op jit(solution)/shard_map/reduce_scatter | solution.py:323
  543.4 179.0 %reduce-scatter.9.cloned.1.call-start = ((), (), s32[]{:S(2)}) async-start(), calls=%async_computation.6 | async-start | bytes 10485760 | tf_op jit(solution)/shard_map/reduce_scatter | solution.py:323
  544.2 312.4 %all-reduce.3.cloned.1.call-start = ((), (), s32[]{:S(2)}) async-start(), calls=%async_computation.12 | async-start | bytes 12582912 | tf_op jit(solution)/shard_map/psum | solution.py:324
  856.6 1.5 copy-start.4
  858.0 1.0 copy-start
  858.2 2.0 copy-start.3
  859.0 1.4 copy-start.1
  859.0 10.4 %slice-start = ((s8[16777216]{0:T(1024)(128)(4,1)}), s8[4194304]{0:T(1024)(128)(4,1)S(1)}, s32[]{:S(2)}) async-start(s8[16777216]{0:T(1024)(128)(4,1)} %bitcast.35), calls=%async_computation.13 | async-start | bytes 8388608
  860.1 2.1 copy-start.2
  860.4 9.1 %slice-start.1 = ((s8[16777216]{0:T(1024)(128)(4,1)}), s8[4194304]{0:T(1024)(128)(4,1)S(1)}, s32[]{:S(2)}) async-start(s8[16777216]{0:T(1024)(128)(4,1)} %bitcast.35), calls=%async_computation.14 | async-start | bytes 8388608
  862.2 1.5 slice-start.5
  862.2 1.8 slice-start.7
  862.5 7.0 slice-start.2
  862.7 2.7 slice-start.4
  862.7 2.9 slice-start.6
  866.5 3.7 slice-start.3
Sparse Core Ops, SparseCore 0:
  10.1 35.2 all-gather.8
  47.5 20.4 all-gather.10
  70.1 32.3 all-gather.12
  104.5 20.4 all-gather.14
  280.1 40.0 reduce-scatter.6
  542.8 39.9 reduce-scatter.4
  586.0 66.9 reduce-scatter.10
  655.5 66.9 reduce-scatter.8
  726.4 130.1 all-reduce.2
